TPU v7x, 32 devices: a whole 2x2x4 slice. The times are simulated.
32 devices in a mesh: mem: 4 (over z), hor: 2 (over x), grp: 4 (over y, core).
Axes of the slice: x: 2, y: 2, z: 4, core: 2. Of those that a mesh axis runs over, the one named last changes fastest.
Arguments:
- ensemble: float32 [128, 2, 32, 1024], P(('mem', 'grp'), None, None, 'hor'), may hold values from -1 to 1
- coupling: float32 [32, 32], replicated, may hold values from -1 to 1
- obs_column: int32 [2, 16, 2, 512], P(None, ('mem', 'grp'), 'hor'), may hold values from 0 to 511
- obs_level: int32 [2, 16, 2, 512], P(None, ('mem', 'grp'), 'hor'), may hold values from 0 to 1
- obs_value: float32 [2, 16, 2, 512], P(None, ('mem', 'grp'), 'hor'), may hold values from -6 to 6
- obs_error: float32 [2, 16, 2, 512], P(None, ('mem', 'grp'), 'hor'), may hold values from 0.25 to 4
- obs_live: int32 [2, 16, 2, 512], P(None, ('mem', 'grp'), 'hor'), may hold values 0 or 1
- partners: int32 [16, 2, 2], P(('mem', 'grp'), 'hor'), may hold values from 0 to 15, as said below
Outputs:
- analysed: float32 [128, 2, 32, 1024], P(('mem', 'grp'), None, None, 'hor')
Inputs may be any that keep to these rules, and one draw needn't show every extreme that they name: `partners`: each row holds 2 different slab numbers, none of them the row's own slab.
All inputs are finite; a program needn't handle non-finite values. No bound on the sum of `obs_live` on one device may be relied on, other than what follows from the above.
Results may differ from a plain program's by a relative error of at most 0.0003.
Values sent between devices are 32-bit elements; how exact they have to be, the bound alone decides.
A program may use at most 64 MiB of HBM per device.

v0:
```python
import functools

import jax
import jax.numpy as jnp
from jax import lax
from jax.experimental import pallas as pl
from jax.experimental.pallas import tpu as pltpu
from jax.sharding import PartitionSpec as P

SUBSTEPS = 4
ROOT_STEPS = 8
MESH = pl.DeviceIdType.MESH


time_step = 0.2


def sent(piece, axis, pairs):
    width = piece.shape[-1]
    packed = jnp.moveaxis(piece, -1, 0).reshape(width, -1)
    moved = lax.ppermute(packed, axis, pairs)
    return jnp.moveaxis(moved.reshape((width,) + piece.shape[:-1]), 0, -1)


def with_halo(block, axis, width):
    count = lax.axis_size(axis)
    forward = [(i, (i + 1) % count) for i in range(count)]
    backward = [(target, source) for source, target in forward]
    low = sent(block[..., block.shape[-1] - width :], axis, forward)
    high = sent(block[..., :width], axis, backward)
    return jnp.concatenate([low, block, high], axis=-1)


def centred(field):
    return (field[..., 2:] - field[..., :-2]) * 0.5


def substep(velocity, height, coupling):
    pressure = jnp.einsum("lk,mkc->mlc", coupling, height, precision=lax.Precision.HIGHEST)
    inner = velocity[..., 1:-1]
    moved = inner - time_step * (inner * centred(velocity) + centred(pressure))
    fluxes = moved * height[..., 1:-1]
    height_new = height[..., 2:-2] - time_step * centred(fluxes)
    return (moved[..., 1:-1], height_new)


def advance(members, coupling):
    extended = with_halo(members, "hor", 2 * SUBSTEPS)
    velocity, height = (extended[:, 0], extended[:, 1])
    for step_index in range(SUBSTEPS):
        velocity, height = substep(velocity, height, coupling)
    members = jnp.stack([velocity, height], axis=1)
    return members


def to_patches(members, mem_count, grp_count):
    block, fields, levels, cells = members.shape
    slab_count = mem_count * grp_count
    thin = levels // slab_count
    shaped = members.reshape(1, block, fields, slab_count, thin, cells)
    moved = lax.all_to_all(shaped, ("mem", "grp"), split_axis=3, concat_axis=0, tiled=True)
    return moved.reshape(slab_count * block, fields, thin, cells)


def from_patches(patch, mem_count, grp_count):
    width, fields, thin, cells = patch.shape
    slab_count = mem_count * grp_count
    block = width // slab_count
    shaped = patch.reshape(slab_count, block, fields, 1, thin, cells)
    moved = lax.all_to_all(shaped, ("mem", "grp"), split_axis=0, concat_axis=3, tiled=True)
    return moved.reshape(block, fields, slab_count * thin, cells)


def split(value):
    high = value.astype(jnp.bfloat16)
    return high, (value - high.astype(jnp.float32)).astype(jnp.bfloat16)


def product(left, right, across=0):
    dims = (((1,), (across,)), ((), ()))

    def one(a, b):
        return lax.dot_general(a, b, dims, preferred_element_type=jnp.float32)

    left_high, left_low = split(left)
    right_high, right_low = split(right)
    return one(left_high, right_high) + (one(left_high, right_low) + one(left_low, right_high))


def analysis(
    sizes, count,
    seen_ref, value_ref, error_ref, live_ref, blend_ref, flat_ref, out_ref,
    own, column, partial, arrived, peers_blend,
    send_a, recv_a, send_b, recv_b, send_c, recv_c,
):
    mem_count, grp_count = sizes
    mem = lax.axis_index("mem")
    grp = lax.axis_index("grp")

    def mem_peer(step):
        return lax.rem(mem + step, mem_count)

    def grp_peer(step):
        return lax.rem(grp + step, grp_count)

    barrier = pltpu.get_barrier_semaphore()
    for step in range(1, mem_count):
        pl.semaphore_signal(barrier, inc=1, device_id={"mem": mem_peer(step)}, device_id_type=MESH)
    for step in range(1, grp_count):
        pl.semaphore_signal(barrier, inc=1, device_id={"grp": grp_peer(step)}, device_id_type=MESH)

    width = seen_ref.shape[0]
    seen = seen_ref[...]
    average = jnp.mean(seen, axis=0, keepdims=True)
    anomalies = seen - average
    weight = live_ref[...].astype(jnp.float32) / error_ref[...]
    pull = weight * (value_ref[...] - average)
    rows = jnp.concatenate(
        [anomalies * weight, jnp.broadcast_to(pull, (8, pull.shape[1]))], axis=0
    )
    own[...] = product(rows, anomalies, 1)

    pl.semaphore_wait(barrier, mem_count + grp_count - 2)
    blends = []
    for step in range(1, grp_count):
        copy = pltpu.make_async_remote_copy(
            src_ref=blend_ref, dst_ref=peers_blend.at[step - 1],
            send_sem=send_b.at[step - 1], recv_sem=recv_b.at[step - 1],
            device_id={"grp": grp_peer(step)}, device_id_type=MESH,
        )
        copy.start()
        blends.append(copy)
    gathers = []
    for step in range(1, mem_count):
        copy = pltpu.make_async_remote_copy(
            src_ref=own, dst_ref=column.at[step - 1],
            send_sem=send_a.at[step - 1], recv_sem=recv_a.at[step - 1],
            device_id={"mem": mem_peer(step)}, device_id_type=MESH,
        )
        copy.start()
        gathers.append(copy)
    for copy in blends:
        copy.wait()
    lanes = lax.broadcasted_iota(jnp.int32, (1, blend_ref.shape[1]), 1)

    def share(row, step):
        place = lax.rem(mem + mem_count - step, mem_count) * grp_count + grp
        return jnp.sum(jnp.where(lanes == place, row[0:1], 0.0), axis=1, keepdims=True)

    for copy in gathers:
        copy.wait()

    def blended_for(row):
        total = share(row, 0) * own[...]
        for step in range(1, mem_count):
            total = total + share(row, step) * column[step - 1]
        return total

    returns = []
    for step in range(1, grp_count):
        partial[step - 1] = blended_for(peers_blend[step - 1])
        copy = pltpu.make_async_remote_copy(
            src_ref=partial.at[step - 1], dst_ref=arrived.at[step - 1],
            send_sem=send_c.at[step - 1], recv_sem=recv_c.at[step - 1],
            device_id={"grp": grp_peer(grp_count - step)}, device_id_type=MESH,
        )
        copy.start()
        returns.append(copy)
    total = blended_for(blend_ref[...])
    flat = flat_ref[...]
    flat_average = jnp.mean(flat, axis=0, keepdims=True)
    for copy in returns:
        copy.wait()
    for step in range(1, grp_count):
        total = total + arrived[step - 1]

    total = total / (count + 1.0)
    square = (width, width)
    identity = (
        lax.broadcasted_iota(jnp.int32, square, 0) == lax.broadcasted_iota(jnp.int32, square, 1)
    ).astype(jnp.float32)
    blended = (width - 1.0) * identity + total[:width]
    bvector = total[width:]
    squares = jnp.sum(jnp.sum(blended * blended, axis=1, keepdims=True), axis=0, keepdims=True)
    frobenius = jnp.sqrt(squares)
    iterate = blended / frobenius
    newton = 1.5 * identity - 0.5 * iterate
    inverse_root = newton
    for step in range(1, ROOT_STEPS):
        iterate = product(newton, iterate)
        newton = 1.5 * identity - 0.5 * product(inverse_root, iterate)
        inverse_root = product(newton, inverse_root)
    spread = inverse_root * (jnp.sqrt(width - 1.0) / jnp.sqrt(frobenius))
    inner = product(bvector, inverse_root)
    mean_weight = product(inner, inverse_root) / frobenius
    transposed = spread + mean_weight[0:1]
    out_ref[...] = flat_average + product(transposed, flat - flat_average)


def analysed(sizes, count, seen, value, error, live, blend, flat):
    width = seen.shape[0]
    mem_count, grp_count = sizes
    tall = (width + 8, width)
    vmem = pl.BlockSpec(memory_space=pltpu.VMEM)
    dma = pltpu.SemaphoreType.DMA
    return pl.pallas_call(
        functools.partial(analysis, sizes, count),
        out_shape=jax.ShapeDtypeStruct(flat.shape, jnp.float32),
        in_specs=[vmem] * 6,
        out_specs=vmem,
        scratch_shapes=[
            pltpu.VMEM(tall, jnp.float32),
            pltpu.VMEM((mem_count - 1,) + tall, jnp.float32),
            pltpu.VMEM((grp_count - 1,) + tall, jnp.float32),
            pltpu.VMEM((grp_count - 1,) + tall, jnp.float32),
            pltpu.VMEM((grp_count - 1,) + blend.shape, jnp.float32),
            dma((mem_count - 1,)), dma((mem_count - 1,)),
            dma((grp_count - 1,)), dma((grp_count - 1,)),
            dma((grp_count - 1,)), dma((grp_count - 1,)),
        ],
        compiler_params=pltpu.CompilerParams(collective_id=0, has_side_effects=True),
    )(seen, value[None], error[None], live[None], blend, flat)


def shards(ensemble, coupling, obs_column, obs_level, obs_value, obs_error, obs_live, partners):
    mem_count = lax.axis_size("mem")
    grp_count = lax.axis_size("grp")
    slab_count = mem_count * grp_count
    own_slab = lax.axis_index("mem") * grp_count + lax.axis_index("grp")
    lanes = max(128, -(-slab_count // 128) * 128)
    slab_numbers = jnp.arange(lanes, dtype=jnp.int32)
    chosen = partners[0, 0]
    count = chosen.shape[0]
    blend_weights = (slab_numbers == own_slab).astype(jnp.float32)
    blend_weights = blend_weights + jnp.sum(
        (slab_numbers[:, None] == chosen[None, :]).astype(jnp.float32), axis=1
    )
    blend = jnp.broadcast_to(blend_weights, (8, lanes))
    width = ensemble.shape[0] * slab_count
    cells = ensemble.shape[3]
    members = ensemble
    for cycle_index in range(obs_column.shape[0]):
        members = advance(members, coupling)
        patch = to_patches(members, mem_count, grp_count)
        place = obs_level[cycle_index, 0, 0] * cells + obs_column[cycle_index, 0, 0]
        observed = jnp.take(patch[:, 1].reshape(width, -1), place, axis=1)
        flat = analysed(
            (mem_count, grp_count), count, observed,
            obs_value[cycle_index, 0, 0], obs_error[cycle_index, 0, 0],
            obs_live[cycle_index, 0, 0], blend, patch.reshape(width, -1),
        )
        members = from_patches(flat.reshape(patch.shape), mem_count, grp_count)
    return members


def solution(mesh):
    in_specs = (
        P(("mem", "grp"), None, None, "hor"),
        P(),
        P(None, ("mem", "grp"), "hor", None),
        P(None, ("mem", "grp"), "hor", None),
        P(None, ("mem", "grp"), "hor", None),
        P(None, ("mem", "grp"), "hor", None),
        P(None, ("mem", "grp"), "hor", None),
        P(("mem", "grp"), "hor", None),
    )
    out_specs = P(("mem", "grp"), None, None, "hor")
    return jax.shard_map(shards, mesh=mesh, in_specs=in_specs, out_specs=out_specs, check_vma=False)
```

profile of v0, /device:TPU:1, one launch (start us, length us, event | category | flops | bytes accessed | tf_op | source)
XLA Modules:
  0.0 204.7 jit_solution(12337920178668115008)
XLA Ops:
  0.0 1.2 fusion.82
  1.4 2.1 %collective-permute-start = (f32[8,512]{1,0:T(8,128)S(1)}, f32[8,512]{1,0:T(8,128)S(1)}, u32[]{:S(2)}, u32[]{:S(2)}) collective-permute-start(f32[8,512]{1,0:T(8,128)S(1)} %copy.89), channel_id=1, source_target_pairs={{0,4},{4,0},{1,5},{5,1},{2,6},{6,2},{3,7},{7,3},{8,12},{12,8},{9,1... | collective-permute-start | bytes 49160 | tf_op jit(solution)/shard_map/ppermute | solution.py:21
  3.6 1.0 collective-permute-done
  4.8 1.3 collective-permute-done.1
  6.4 0.5 pad_maximum_fusion
  7.0 0.7 convolution_bitcast_fusion.7
  7.7 0.7 slice_multiply_fusion.7
  8.4 0.4 fusion.51
  8.9 0.7 convolution_bitcast_fusion.6
  9.5 0.9 slice_multiply_fusion.6
  10.5 0.4 fusion.43
  10.9 0.7 convolution_bitcast_fusion.5
  11.6 0.9 slice_multiply_fusion.5
  12.9 0.7 convolution_bitcast_fusion.4
  13.6 0.9 slice_multiply_fusion.4
  15.7 1.1 pad_maximum_fusion.2
  16.8 8.1 %all-to-all-start = ((f32[1,8,2,16,2,512]{5,1,4,2,0,3:T(8,128)}), f32[1,8,2,16,2,512]{5,1,4,2,0,3:T(8,128)S(1)}, u32[]{:S(2)}, u32[]{:S(2)}) async-start(f32[1,8,2,16,2,512]{5,1,4,2,0,3:T(8,128)} %pad_maximum_fusion.2), calls=%async_computation | async-start | bytes 2097152 | tf_op jit(solution)/shard_map/all_to_all | solution.py:61
  25.1 0.6 slice_bitcast_fusion.6
  25.7 0.6 slice_bitcast_fusion.7
  26.3 21.8 %all-to-all-done = f32[1,8,2,16,2,512]{5,1,4,2,0,3:T(8,128)S(1)} async-done(((f32[1,8,2,16,2,512]{5,1,4,2,0,3:T(8,128)}), f32[1,8,2,16,2,512]{5,1,4,2,0,3:T(8,128)S(1)}, u32[]{:S(2)}, u32[]{:S(2)}) %all-to-all-start) | async-done | bytes 1048608 | tf_op jit(solution)/shard_map/all_to_all | solution.py:61
  48.4 1.0 gather_fusion
  49.6 1.1 copy.99
  50.7 0.7 select_bitcast_fusion.1.seen_ref
  51.4 0.6 broadcast_in_dim.13.blend_ref
  52.0 20.8 %shard_map.82 = f32[128,2048]{1,0:T(8,128)} custom-call(f32[128,512]{1,0:T(8,128)} %select_bitcast_fusion.1.seen_ref, f32[1,512]{1,0:T(1,128)} %get-tuple-element.42.value_ref, f32[1,512]{1,0:T(1,128)} %get-tuple-element.39.error_ref, s32[1,512]{1,0:T(1,128)} %get-tuple-element.37.live_ref, f32[8,128]{1,0:T(8,128)} %broadcast_in_dim.13.blend_ref, ...), custom_call_target="tpu_custom_call" | custom-call | tf_op jit(solution)/shard_map/pallas_call | solution.py:206
  72.8 30.6 %all_to_all.60 = f32[16,8,2,1,2,512]{5,1,4,2,3,0:T(8,128)S(1)} all-to-all(f32[16,8,2,1,2,512]{5,1,4,2,3,0:T(8,128)} %bitcast.133), channel_id=1, replica_groups=mesh['mem'=4,'hor'=2,'grp'=4] {'mem','grp'}, dimensions={0} | all-to-all | bytes 2097152 | tf_op jit(solution)/shard_map/all_to_all | solution.py:70
  103.4 0.8 copy.101
  104.2 0.7 reshape.69
  105.9 1.3 collective-permute-start.3
  107.2 1.3 collective-permute-done.2
  109.0 0.5 pad_maximum_fusion.1
  109.6 0.7 convolution_bitcast_fusion.3
  110.2 0.7 slice_multiply_fusion.3
  111.4 0.7 convolution_bitcast_fusion.2
  112.1 0.9 slice_multiply_fusion.2
  113.4 0.7 convolution_bitcast_fusion.1
  114.1 0.9 slice_multiply_fusion.1
  115.5 0.7 convolution_bitcast_fusion
  116.1 0.9 slice_multiply_fusion
  118.2 1.1 pad_maximum_fusion.3
  119.3 5.7 %all-to-all-start.2 = ((f32[1,8,2,16,2,512]{5,1,4,2,0,3:T(8,128)}), f32[1,8,2,16,2,512]{5,1,4,2,0,3:T(8,128)S(1)}, u32[]{:S(2)}, u32[]{:S(2)}) async-start(f32[1,8,2,16,2,512]{5,1,4,2,0,3:T(8,128)} %pad_maximum_fusion.3), calls=%async_computation.2 | async-start | bytes 2097152 | tf_op jit(solution)/shard_map/all_to_all | solution.py:61
  125.1 23.1 %all-to-all-done.2 = f32[1,8,2,16,2,512]{5,1,4,2,0,3:T(8,128)S(1)} async-done(((f32[1,8,2,16,2,512]{5,1,4,2,0,3:T(8,128)}), f32[1,8,2,16,2,512]{5,1,4,2,0,3:T(8,128)S(1)}, u32[]{:S(2)}, u32[]{:S(2)}) %all-to-all-start.2) | async-done | bytes 1048608 | tf_op jit(solution)/shard_map/all_to_all | solution.py:61
  148.6 1.0 gather_fusion.1
  149.8 1.1 copy.111
  150.8 0.7 select_bitcast_fusion.seen_ref
  151.6 20.8 %shard_map.83 = f32[128,2048]{1,0:T(8,128)} custom-call(f32[128,512]{1,0:T(8,128)} %select_bitcast_fusion.seen_ref, f32[1,512]{1,0:T(1,128)} %get-tuple-element.43.value_ref, f32[1,512]{1,0:T(1,128)} %get-tuple-element.38.error_ref, s32[1,512]{1,0:T(1,128)} %get-tuple-element.36.live_ref, f32[8,128]{1,0:T(8,128)} %broadcast_in_dim.13.blend_ref, ...), custom_call_target="tpu_custom_call" | custom-call | tf_op jit(solution)/shard_map/pallas_call | solution.py:206
  172.4 30.6 %all_to_all.61 = f32[16,8,2,1,2,512]{5,1,4,2,3,0:T(8,128)S(1)} all-to-all(f32[16,8,2,1,2,512]{5,1,4,2,3,0:T(8,128)} %bitcast.132), channel_id=1, replica_groups=mesh['mem'=4,'hor'=2,'grp'=4] {'mem','grp'}, dimensions={0} | all-to-all | bytes 2097152 | tf_op jit(solution)/shard_map/all_to_all | solution.py:70
  203.1 1.6 copy.114
  (66 shorter events, 7.5 us)
Async XLA Ops:
  0.0 7.0 %copy-start = (f32[32,32]{1,0:T(8,128)S(1)}, f32[32,32]{1,0:T(8,128)}, u32[]{:S(2)}) copy-start(f32[32,32]{1,0:T(8,128)} %param.11) | copy-start | bytes 12292
  0.0 6.4 %copy-start.1 = (f32[8,2,32,512]{3,2,1,0:T(8,128)S(1)}, f32[8,2,32,512]{3,2,1,0:T(8,128)}, u32[]{:S(2)}) copy-start(f32[8,2,32,512]{3,2,1,0:T(8,128)} %param.10) | copy-start | bytes 3145732
  1.4 3.2 %collective-permute-start = (f32[8,512]{1,0:T(8,128)S(1)}, f32[8,512]{1,0:T(8,128)S(1)}, u32[]{:S(2)}, u32[]{:S(2)}) collective-permute-start(f32[8,512]{1,0:T(8,128)S(1)} %copy.89), channel_id=1, source_target_pairs={{0,4},{4,0},{1,5},{5,1},{2,6},{6,2},{3,7},{7,3},{8,12},{12,8},{9,1... | collective-permute-start | bytes 49160 | tf_op jit(solution)/shard_map/ppermute | solution.py:21
  3.5 2.6 %collective-permute-start.1 = (f32[8,512]{1,0:T(8,128)S(1)}, f32[8,512]{1,0:T(8,128)S(1)}, u32[]{:S(2)}, u32[]{:S(2)}) collective-permute-start(f32[8,512]{1,0:T(8,128)S(1)} %copy.91), channel_id=1, source_target_pairs={{4,0},{0,4},{5,1},{1,5},{6,2},{2,6},{7,3},{3,7},{12,8},{8,12},{13,... | collective-permute-start | bytes 49160 | tf_op jit(solution)/shard_map/ppermute | solution.py:21
  16.8 8.1 %copy-start.2 = (s32[2,1,1,512]{3,2,1,0:T(1,128)S(1)}, s32[2,1,1,512]{3,2,1,0:T(1,128)}, u32[]{:S(2)}) copy-start(s32[2,1,1,512]{3,2,1,0:T(1,128)} %param.12) | copy-start | bytes 12292
  16.8 8.1 %copy-start.3 = (s32[2,1,1,512]{3,2,1,0:T(1,128)S(1)}, s32[2,1,1,512]{3,2,1,0:T(1,128)}, u32[]{:S(2)}) copy-start(s32[2,1,1,512]{3,2,1,0:T(1,128)} %param.13) | copy-start | bytes 12292
  16.8 8.2 %copy-start.7 = (s32[1,1,2]{2,1,0:T(1,128)S(1)}, s32[1,1,2]{2,1,0:T(1,128)}, u32[]{:S(2)}) copy-start(s32[1,1,2]{2,1,0:T(1,128)} %param.17) | copy-start | bytes 28
  16.8 8.3 %copy-start.4 = (s32[2,1,1,512]{3,2,1,0:T(1,128)S(1)}, s32[2,1,1,512]{3,2,1,0:T(1,128)}, u32[]{:S(2)}) copy-start(s32[2,1,1,512]{3,2,1,0:T(1,128)} %param.16) | copy-start | bytes 12292
  16.8 8.9 %copy-start.5 = (f32[2,1,1,512]{3,2,1,0:T(1,128)S(1)}, f32[2,1,1,512]{3,2,1,0:T(1,128)}, u32[]{:S(2)}) copy-start(f32[2,1,1,512]{3,2,1,0:T(1,128)} %param.15) | copy-start | bytes 12292
  16.8 8.9 %copy-start.6 = (f32[2,1,1,512]{3,2,1,0:T(1,128)S(1)}, f32[2,1,1,512]{3,2,1,0:T(1,128)}, u32[]{:S(2)}) copy-start(f32[2,1,1,512]{3,2,1,0:T(1,128)} %param.14) | copy-start | bytes 12292
  16.8 31.3 %all-to-all-start = ((f32[1,8,2,16,2,512]{5,1,4,2,0,3:T(8,128)}), f32[1,8,2,16,2,512]{5,1,4,2,0,3:T(8,128)S(1)}, u32[]{:S(2)}, u32[]{:S(2)}) async-start(f32[1,8,2,16,2,512]{5,1,4,2,0,3:T(8,128)} %pad_maximum_fusion.2), calls=%async_computation | async-start | bytes 2097152 | tf_op jit(solution)/shard_map/all_to_all | solution.py:61
  105.4 3.1 %collective-permute-start.2 = (f32[8,512]{1,0:T(8,128)S(1)}, f32[8,512]{1,0:T(8,128)S(1)}, u32[]{:S(2)}, u32[]{:S(2)}) collective-permute-start(f32[8,512]{1,0:T(8,128)S(1)} %reshape.70), channel_id=1, source_target_pairs={{0,4},{4,0},{1,5},{5,1},{2,6},{6,2},{3,7},{7,3},{8,12},{12,8},{9,1... | collective-permute-start | bytes 49160 | tf_op jit(solution)/shard_map/ppermute | solution.py:21
  105.9 2.8 %collective-permute-start.3 = (f32[8,512]{1,0:T(8,128)S(1)}, f32[8,512]{1,0:T(8,128)S(1)}, u32[]{:S(2)}, u32[]{:S(2)}) collective-permute-start(f32[8,512]{1,0:T(8,128)S(1)} %reshape.72), channel_id=1, source_target_pairs={{4,0},{0,4},{5,1},{1,5},{6,2},{2,6},{7,3},{3,7},{12,8},{8,12},{13,... | collective-permute-start | bytes 49160 | tf_op jit(solution)/shard_map/ppermute | solution.py:21
  119.3 28.9 %all-to-all-start.2 = ((f32[1,8,2,16,2,512]{5,1,4,2,0,3:T(8,128)}), f32[1,8,2,16,2,512]{5,1,4,2,0,3:T(8,128)S(1)}, u32[]{:S(2)}, u32[]{:S(2)}) async-start(f32[1,8,2,16,2,512]{5,1,4,2,0,3:T(8,128)} %pad_maximum_fusion.3), calls=%async_computation.2 | async-start | bytes 2097152 | tf_op jit(solution)/shard_map/all_to_all | solution.py:61
where the time goes:
time: 205 us
  blocking collectives  61.2 us (30%)
  waiting for transfers between devices  48.5 us (24%)
  Pallas kernels  41.6 us (20%)
  starting transfers between devices  17.5 us (9%)
  local copies, waits for them, and re-layouts  15 us (7%)
  other arithmetic  14.8 us (7%)
  matrix products  5.44 us (3%)
    all_to_all x2, blocking collectives, from_patches(): lax.all_to_all(shaped, ('mem', 'grp'), split_axis=0, concat_axis=3, tiled...  61.2 us
    all_to_all x2, waiting for transfers between devices, to_patches(): lax.all_to_all(shaped, ('mem', 'grp'), split_axis=3, concat_axis=0, tiled...  44.9 us
    pallas_call x2, Pallas kernels, analysed(): pl.pallas_call(functools.partial(analysis, sizes, count), out_shape=jax.S...  41.6 us
    all_to_all x2, starting transfers between devices, to_patches(): lax.all_to_all(shaped, ('mem', 'grp'), split_axis=3, concat_axis=0, tiled...  13.8 us
    mul x8, other arithmetic, substep(): fluxes = moved * height[..., 1:-1]  6.95 us
    dot_general x8, matrix products, substep(): jnp.einsum('lk,mkc->mlc', coupling, height, precision=lax.Precision.HIGHEST)  5.44 us
  transfers between devices with their start and end apart: 6, of which 5 were waited for; matrix products, arithmetic and copies ran while one was open for 1% of the time, Pallas kernels for 0%

commit v1 on v0

--- a/solution.py
+++ b/solution.py
@@ -49,26 +49,12 @@
     velocity, height = (extended[:, 0], extended[:, 1])
     for step_index in range(SUBSTEPS):
         velocity, height = substep(velocity, height, coupling)
-    members = jnp.stack([velocity, height], axis=1)
-    return members
-
-
-def to_patches(members, mem_count, grp_count):
-    block, fields, levels, cells = members.shape
-    slab_count = mem_count * grp_count
-    thin = levels // slab_count
-    shaped = members.reshape(1, block, fields, slab_count, thin, cells)
-    moved = lax.all_to_all(shaped, ("mem", "grp"), split_axis=3, concat_axis=0, tiled=True)
-    return moved.reshape(slab_count * block, fields, thin, cells)
-
-
-def from_patches(patch, mem_count, grp_count):
-    width, fields, thin, cells = patch.shape
-    slab_count = mem_count * grp_count
-    block = width // slab_count
-    shaped = patch.reshape(slab_count, block, fields, 1, thin, cells)
-    moved = lax.all_to_all(shaped, ("mem", "grp"), split_axis=0, concat_axis=3, tiled=True)
-    return moved.reshape(block, fields, slab_count * thin, cells)
+    return velocity, height
+
+
+def to_slabs(field, slab_count):
+    block, levels, cells = field.shape
+    return field.reshape(block, slab_count, -1).transpose(1, 0, 2)
 
 
 def split(value):
@@ -89,9 +75,9 @@
 
 def analysis(
     sizes, count,
-    seen_ref, value_ref, error_ref, live_ref, blend_ref, flat_ref, out_ref,
-    own, column, partial, arrived, peers_blend,
-    send_a, recv_a, send_b, recv_b, send_c, recv_c,
+    seen_ref, value_ref, error_ref, live_ref, blend_ref, height_ref, velocity_ref, out_ref,
+    own, column, partial, arrived, peers_blend, gathered, updated, returned,
+    send_a, recv_a, send_b, recv_b, send_c, recv_c, send_d, recv_d, send_e, recv_e,
 ):
     mem_count, grp_count = sizes
     mem = lax.axis_index("mem")
@@ -104,10 +90,29 @@
         return lax.rem(grp + step, grp_count)
 
     barrier = pltpu.get_barrier_semaphore()
-    for step in range(1, mem_count):
-        pl.semaphore_signal(barrier, inc=1, device_id={"mem": mem_peer(step)}, device_id_type=MESH)
-    for step in range(1, grp_count):
-        pl.semaphore_signal(barrier, inc=1, device_id={"grp": grp_peer(step)}, device_id_type=MESH)
+    slab = mem * grp_count + grp
+    peers = []
+    for mem_step in range(mem_count):
+        for grp_step in range(grp_count):
+            if mem_step + grp_step > 0:
+                peers.append((mem_peer(mem_step), grp_peer(grp_step)))
+    for one, other in peers:
+        pl.semaphore_signal(
+            barrier, inc=1, device_id={"mem": one, "grp": other}, device_id_type=MESH
+        )
+
+    def exchange(source, target, send_sem, recv_sem):
+        copies = []
+        for at, (one, other) in enumerate(peers):
+            copy = pltpu.make_async_remote_copy(
+                src_ref=source.at[one * grp_count + other], dst_ref=target.at[slab],
+                send_sem=send_sem.at[at], recv_sem=recv_sem.at[at],
+                device_id={"mem": one, "grp": other}, device_id_type=MESH,
+            )
+            copy.start()
+            copies.append(copy)
+        return copies
+
 
     width = seen_ref.shape[0]
     seen = seen_ref[...]
@@ -120,7 +125,7 @@
     )
     own[...] = product(rows, anomalies, 1)
 
-    pl.semaphore_wait(barrier, mem_count + grp_count - 2)
+    pl.semaphore_wait(barrier, mem_count * grp_count - 1)
     blends = []
     for step in range(1, grp_count):
         copy = pltpu.make_async_remote_copy(
@@ -167,8 +172,8 @@
         copy.start()
         returns.append(copy)
     total = blended_for(blend_ref[...])
-    flat = flat_ref[...]
-    flat_average = jnp.mean(flat, axis=0, keepdims=True)
+    outward = exchange(velocity_ref, gathered, send_d, recv_d)
+    gathered[slab] = velocity_ref[slab]
     for copy in returns:
         copy.wait()
     for step in range(1, grp_count):
@@ -194,10 +199,25 @@
     inner = product(bvector, inverse_root)
     mean_weight = product(inner, inverse_root) / frobenius
     transposed = spread + mean_weight[0:1]
-    out_ref[...] = flat_average + product(transposed, flat - flat_average)
-
-
-def analysed(sizes, count, seen, value, error, live, blend, flat):
+
+    def update(flat, field):
+        flat_average = jnp.mean(flat, axis=0, keepdims=True)
+        result = flat_average + product(transposed, flat - flat_average)
+        updated[field] = result.reshape(updated.shape[1:])
+        copies = exchange(updated.at[field], returned.at[field], send_e.at[field], recv_e.at[field])
+        returned[field, slab] = updated[field, slab]
+        return copies
+
+    back = update(height_ref[...], 1)
+    for copy in outward:
+        copy.wait()
+    back = back + update(gathered[...].reshape(height_ref.shape), 0)
+    for copy in back:
+        copy.wait()
+    out_ref[...] = returned[...]
+
+
+def analysed(sizes, count, seen, value, error, live, blend, height, velocity):
     width = seen.shape[0]
     mem_count, grp_count = sizes
     tall = (width + 8, width)
@@ -205,8 +225,8 @@
     dma = pltpu.SemaphoreType.DMA
     return pl.pallas_call(
         functools.partial(analysis, sizes, count),
-        out_shape=jax.ShapeDtypeStruct(flat.shape, jnp.float32),
-        in_specs=[vmem] * 6,
+        out_shape=jax.ShapeDtypeStruct((2,) + velocity.shape, jnp.float32),
+        in_specs=[vmem] * 7,
         out_specs=vmem,
         scratch_shapes=[
             pltpu.VMEM(tall, jnp.float32),
@@ -214,12 +234,17 @@
             pltpu.VMEM((grp_count - 1,) + tall, jnp.float32),
             pltpu.VMEM((grp_count - 1,) + tall, jnp.float32),
             pltpu.VMEM((grp_count - 1,) + blend.shape, jnp.float32),
+            pltpu.VMEM(velocity.shape, jnp.float32),
+            pltpu.VMEM((2,) + velocity.shape, jnp.float32),
+            pltpu.VMEM((2,) + velocity.shape, jnp.float32),
             dma((mem_count - 1,)), dma((mem_count - 1,)),
             dma((grp_count - 1,)), dma((grp_count - 1,)),
             dma((grp_count - 1,)), dma((grp_count - 1,)),
+            dma((mem_count * grp_count - 1,)), dma((mem_count * grp_count - 1,)),
+            dma((2, mem_count * grp_count - 1)), dma((2, mem_count * grp_count - 1)),
         ],
         compiler_params=pltpu.CompilerParams(collective_id=0, has_side_effects=True),
-    )(seen, value[None], error[None], live[None], blend, flat)
+    )(seen, value[None], error[None], live[None], blend, height, velocity)
 
 
 def shards(ensemble, coupling, obs_column, obs_level, obs_value, obs_error, obs_live, partners):
@@ -240,16 +265,19 @@
     cells = ensemble.shape[3]
     members = ensemble
     for cycle_index in range(obs_column.shape[0]):
-        members = advance(members, coupling)
-        patch = to_patches(members, mem_count, grp_count)
+        velocity, height = advance(members, coupling)
+        heights = lax.all_to_all(
+            to_slabs(height, slab_count), ("mem", "grp"), split_axis=0, concat_axis=0, tiled=True
+        ).reshape(width, -1)
         place = obs_level[cycle_index, 0, 0] * cells + obs_column[cycle_index, 0, 0]
-        observed = jnp.take(patch[:, 1].reshape(width, -1), place, axis=1)
-        flat = analysed(
+        observed = jnp.take(heights, place, axis=1)
+        result = analysed(
             (mem_count, grp_count), count, observed,
             obs_value[cycle_index, 0, 0], obs_error[cycle_index, 0, 0],
-            obs_live[cycle_index, 0, 0], blend, patch.reshape(width, -1),
-        )
-        members = from_patches(flat.reshape(patch.shape), mem_count, grp_count)
+            obs_live[cycle_index, 0, 0], blend, heights, to_slabs(velocity, slab_count),
+        )
+        shaped = result.reshape(2, slab_count, ensemble.shape[0], -1, cells)
+        members = shaped.transpose(2, 0, 1, 3, 4).reshape(ensemble.shape)
     return members
 
 

time: 205 us -> 178 us (0.87)
  blocking collectives: 61.2 us -> 0 us
  Pallas kernels: 41.6 us -> 93.3 us
  waiting for transfers between devices: 48.5 us -> 27.2 us
  local copies, waits for them, and re-layouts: 15 us -> 18.2 us
    all_to_all x2 -> x0, blocking collectives: 61.2 us -> none  [from_patches(): lax.all_to_all(shaped, ('mem', 'grp'), split_axis=0, concat_axis=3, tiled...]
    pallas_call x2, Pallas kernels: 41.6 us -> 93.3 us  [analysed(): pl.pallas_call(functools.partial(analysis, sizes, count), out_shape=jax.S...]
    all_to_all x2, waiting for transfers between devices: 44.9 us -> 23.7 us  [shards(): lax.all_to_all(to_slabs(height, slab_count), ('mem', 'grp'), split_axis=0...]
    reshape x2 -> x12, local copies, waits for them, and re-layouts: 2.31 us -> 10.2 us  [the longest x8 5.14 us: to_slabs(): return field.reshape(block, slab_count, -1).transpose(1, 0, 2)]
    all_to_all x6 -> x0, local copies, waits for them, and re-layouts: 3.2 us -> none  [the longest x4 2.29 us: to_patches(): lax.all_to_all(shaped, ('mem', 'grp'), split_axis=3, concat_axis=0, tiled...]
    another operation x2 -> x0, other arithmetic: 2.16 us -> none  [advance(): members = jnp.stack([velocity, height], axis=1)]
  transfers between devices with their start and end apart: 6 -> 6, of which waited for: 5 -> 6; matrix products, arithmetic and copies ran while one was open for 1% -> 3% of each run, Pallas kernels for 0% -> 0%
where the time goes in v1:
time: 178 us; the launch traced here: 177 us
  Pallas kernels  93.3 us (52%)
  waiting for transfers between devices  27.2 us (15%)
  starting transfers between devices  19.4 us (11%)
  local copies, waits for them, and re-layouts  18.2 us (10%)
  other arithmetic  12.9 us (7%)
  matrix products  5.43 us (3%)
    pallas_call x2, Pallas kernels, analysed(): pl.pallas_call(functools.partial(analysis, sizes, count), out_shape=jax.S...  93.3 us
    all_to_all x2, waiting for transfers between devices, shards(): lax.all_to_all(to_slabs(height, slab_count), ('mem', 'grp'), split_axis=0...  23.7 us
    all_to_all x2, starting transfers between devices, shards(): lax.all_to_all(to_slabs(height, slab_count), ('mem', 'grp'), split_axis=0...  15.7 us
    mul x8, other arithmetic, substep(): fluxes = moved * height[..., 1:-1]  7.16 us
    dot_general x8, matrix products, substep(): jnp.einsum('lk,mkc->mlc', coupling, height, precision=lax.Precision.HIGHEST)  5.43 us
    reshape x8, local copies, waits for them, and re-layouts, to_slabs(): return field.reshape(block, slab_count, -1).transpose(1, 0, 2)  5.14 us
    reshape x2, local copies, waits for them, and re-layouts, shards(): members = shaped.transpose(2, 0, 1, 3, 4).reshape(ensemble.shape)  4.64 us
    ppermute x4, starting transfers between devices, sent(): moved = lax.ppermute(packed, axis, pairs)  3.68 us
  transfers between devices with their start and end apart: 6, of which 6 were waited for; matrix products, arithmetic and copies ran while one was open for 3% of the time, Pallas kernels for 0%

profile of v1, /device:TPU:1, one launch (start us, length us, event | category | flops | bytes accessed | tf_op | source)
XLA Modules:
  0.0 177.0 jit_solution(15209353822102408208)
XLA Ops:
  0.0 1.2 fusion.82
  1.4 2.1 %collective-permute-start = (f32[8,512]{1,0:T(8,128)S(1)}, f32[8,512]{1,0:T(8,128)S(1)}, u32[]{:S(2)}, u32[]{:S(2)}) collective-permute-start(f32[8,512]{1,0:T(8,128)S(1)} %copy.37), channel_id=1, source_target_pairs={{0,4},{4,0},{1,5},{5,1},{2,6},{6,2},{3,7},{7,3},{8,12},{12,8},{9,1... | collective-permute-start | bytes 49160 | tf_op jit(solution)/shard_map/ppermute | solution.py:21
  3.7 0.8 collective-permute-done
  4.8 1.3 collective-permute-done.1
  6.4 0.5 pad_maximum_fusion
  7.0 0.7 convolution_bitcast_fusion.7
  7.7 0.7 slice_multiply_fusion.7
  8.5 0.4 fusion.53
  8.9 0.7 convolution_bitcast_fusion.6
  9.6 0.9 slice_multiply_fusion.6
  10.5 0.4 fusion.45
  10.9 0.7 convolution_bitcast_fusion.5
  11.6 0.9 slice_multiply_fusion.5
  12.9 0.7 convolution_bitcast_fusion.4
  13.6 0.9 slice_multiply_fusion.4
  15.1 1.1 copy.67
  16.2 7.9 %all-to-all-start = ((f32[16,8,1024]{2,1,0:T(8,128)}), f32[16,8,1024]{2,1,0:T(8,128)S(1)}, u32[]{:S(2)}, u32[]{:S(2)}) async-start(f32[16,8,1024]{2,1,0:T(8,128)} %bitcast.105), calls=%async_computation | async-start | bytes 1048576 | tf_op jit(solution)/shard_map/all_to_all | solution.py:269
  24.2 0.6 slice_bitcast_fusion.6
  24.8 0.6 slice_bitcast_fusion.7
  25.8 1.1 copy.66
  26.9 11.2 %all-to-all-done = f32[16,8,1024]{2,1,0:T(8,128)S(1)} async-done(((f32[16,8,1024]{2,1,0:T(8,128)}), f32[16,8,1024]{2,1,0:T(8,128)S(1)}, u32[]{:S(2)}, u32[]{:S(2)}) %all-to-all-start) | async-done | bytes 524320 | tf_op jit(solution)/shard_map/all_to_all | solution.py:269
  38.3 1.2 gather_fusion
  39.7 0.7 select_bitcast_fusion.1.seen_ref
  40.5 0.6 broadcast_in_dim.13.blend_ref
  41.1 46.7 %shard_map.82 = f32[2,16,8,1024]{3,2,1,0:T(8,128)} custom-call(f32[128,512]{1,0:T(8,128)} %select_bitcast_fusion.1.seen_ref, f32[1,512]{1,0:T(1,128)} %get-tuple-element.38.value_ref, f32[1,512]{1,0:T(1,128)} %get-tuple-element.35.error_ref, s32[1,512]{1,0:T(1,128)} %get-tuple-element.33.live_ref, f32[8,128]{1,0:T(8,128)} %broadcast_in_dim.13.blend_ref, ...), custom_call_target="tpu_custom_call" | custom-call | tf_op jit(solution)/shard_map/pallas_call | solution.py:226
  87.7 1.8 %copy.56 = f32[8,2,32,512]{3,2,0,1:T(8,128)S(1)} copy(f32[8,2,32,512]{3,0,2,1:T(8,128)} %bitcast.111) | data formatting | bytes 2097152 | tf_op jit(solution)/shard_map/reshape | solution.py:280
  90.6 1.3 collective-permute-start.3
  91.8 0.8 collective-permute-done.2
  92.9 0.5 collective-permute-done.3
  93.7 0.5 pad_maximum_fusion.1
  94.2 0.7 convolution_bitcast_fusion.3
  94.9 0.7 slice_multiply_fusion.3
  95.7 0.4 fusion.23
  96.1 0.7 convolution_bitcast_fusion.2
  96.8 0.9 slice_multiply_fusion.2
  97.7 0.4 fusion.15
  98.1 0.7 convolution_bitcast_fusion.1
  98.8 0.9 slice_multiply_fusion.1
  100.1 0.7 convolution_bitcast_fusion
  100.8 1.1 slice_multiply_fusion
  102.5 1.1 copy.65
  103.6 7.7 %all-to-all-start.1 = ((f32[16,8,1024]{2,1,0:T(8,128)}), f32[16,8,1024]{2,1,0:T(8,128)S(1)}, u32[]{:S(2)}, u32[]{:S(2)}) async-start(f32[16,8,1024]{2,1,0:T(8,128)} %bitcast.103), calls=%async_computation.1 | async-start | bytes 1048576 | tf_op jit(solution)/shard_map/all_to_all | solution.py:269
  111.8 1.1 copy.64
  112.9 12.5 %all-to-all-done.1 = f32[16,8,1024]{2,1,0:T(8,128)S(1)} async-done(((f32[16,8,1024]{2,1,0:T(8,128)}), f32[16,8,1024]{2,1,0:T(8,128)S(1)}, u32[]{:S(2)}, u32[]{:S(2)}) %all-to-all-start.1) | async-done | bytes 524320 | tf_op jit(solution)/shard_map/all_to_all | solution.py:269
  125.5 1.0 gather_fusion.1
  126.7 0.7 select_bitcast_fusion.seen_ref
  127.5 46.7 %shard_map.83 = f32[2,16,8,1024]{3,2,1,0:T(8,128)} custom-call(f32[128,512]{1,0:T(8,128)} %select_bitcast_fusion.seen_ref, f32[1,512]{1,0:T(1,128)} %get-tuple-element.39.value_ref, f32[1,512]{1,0:T(1,128)} %get-tuple-element.34.error_ref, s32[1,512]{1,0:T(1,128)} %get-tuple-element.32.live_ref, f32[8,128]{1,0:T(8,128)} %broadcast_in_dim.13.blend_ref, ...), custom_call_target="tpu_custom_call" | custom-call | tf_op jit(solution)/shard_map/pallas_call | solution.py:226
  174.2 2.8 %copy.57 = f32[8,2,32,512]{3,2,1,0:T(8,128)} copy(f32[8,2,32,512]{3,0,2,1:T(8,128)} %bitcast.110) | data formatting | bytes 2097152 | tf_op jit(solution)/shard_map/reshape | solution.py:280
  (62 shorter events, 5.8 us)
Async XLA Ops:
  0.0 7.0 %copy-start = (f32[32,32]{1,0:T(8,128)S(1)}, f32[32,32]{1,0:T(8,128)}, u32[]{:S(2)}) copy-start(f32[32,32]{1,0:T(8,128)} %param.11) | copy-start | bytes 12292
  0.0 6.4 %copy-start.3 = (f32[8,2,32,512]{3,2,1,0:T(8,128)S(1)}, f32[8,2,32,512]{3,2,1,0:T(8,128)}, u32[]{:S(2)}) copy-start(f32[8,2,32,512]{3,2,1,0:T(8,128)} %param.10) | copy-start | bytes 3145732
  0.0 3.6 %copy-start.4 = (s32[2,1,1,512]{3,2,1,0:T(1,128)S(1)}, s32[2,1,1,512]{3,2,1,0:T(1,128)}, u32[]{:S(2)}) copy-start(s32[2,1,1,512]{3,2,1,0:T(1,128)} %param.12) | copy-start | bytes 12292
  0.0 3.6 %copy-start.5 = (s32[2,1,1,512]{3,2,1,0:T(1,128)S(1)}, s32[2,1,1,512]{3,2,1,0:T(1,128)}, u32[]{:S(2)}) copy-start(s32[2,1,1,512]{3,2,1,0:T(1,128)} %param.13) | copy-start | bytes 12292
  0.0 3.6 %copy-start.9 = (s32[1,1,2]{2,1,0:T(1,128)S(1)}, s32[1,1,2]{2,1,0:T(1,128)}, u32[]{:S(2)}) copy-start(s32[1,1,2]{2,1,0:T(1,128)} %param.17) | copy-start | bytes 28
  1.4 3.2 %collective-permute-start = (f32[8,512]{1,0:T(8,128)S(1)}, f32[8,512]{1,0:T(8,128)S(1)}, u32[]{:S(2)}, u32[]{:S(2)}) collective-permute-start(f32[8,512]{1,0:T(8,128)S(1)} %copy.37), channel_id=1, source_target_pairs={{0,4},{4,0},{1,5},{5,1},{2,6},{6,2},{3,7},{7,3},{8,12},{12,8},{9,1... | collective-permute-start | bytes 49160 | tf_op jit(solution)/shard_map/ppermute | solution.py:21
  3.5 2.6 %collective-permute-start.1 = (f32[8,512]{1,0:T(8,128)S(1)}, f32[8,512]{1,0:T(8,128)S(1)}, u32[]{:S(2)}, u32[]{:S(2)}) collective-permute-start(f32[8,512]{1,0:T(8,128)S(1)} %copy.39), channel_id=1, source_target_pairs={{4,0},{0,4},{5,1},{1,5},{6,2},{2,6},{7,3},{3,7},{12,8},{8,12},{13,... | collective-permute-start | bytes 49160 | tf_op jit(solution)/shard_map/ppermute | solution.py:21
  15.1 9.1 %copy-start.6 = (s32[2,1,1,512]{3,2,1,0:T(1,128)S(1)}, s32[2,1,1,512]{3,2,1,0:T(1,128)}, u32[]{:S(2)}) copy-start(s32[2,1,1,512]{3,2,1,0:T(1,128)} %param.16) | copy-start | bytes 12292
  15.1 9.7 %copy-start.7 = (f32[2,1,1,512]{3,2,1,0:T(1,128)S(1)}, f32[2,1,1,512]{3,2,1,0:T(1,128)}, u32[]{:S(2)}) copy-start(f32[2,1,1,512]{3,2,1,0:T(1,128)} %param.15) | copy-start | bytes 12292
  15.1 9.7 %copy-start.8 = (f32[2,1,1,512]{3,2,1,0:T(1,128)S(1)}, f32[2,1,1,512]{3,2,1,0:T(1,128)}, u32[]{:S(2)}) copy-start(f32[2,1,1,512]{3,2,1,0:T(1,128)} %param.14) | copy-start | bytes 12292
  16.2 22.0 %all-to-all-start = ((f32[16,8,1024]{2,1,0:T(8,128)}), f32[16,8,1024]{2,1,0:T(8,128)S(1)}, u32[]{:S(2)}, u32[]{:S(2)}) async-start(f32[16,8,1024]{2,1,0:T(8,128)} %bitcast.105), calls=%async_computation | async-start | bytes 1048576 | tf_op jit(solution)/shard_map/all_to_all | solution.py:269
  38.1 1.4 copy-start.1
  90.0 2.6 %collective-permute-start.2 = (f32[8,512]{1,0:T(8,128)S(1)}, f32[8,512]{1,0:T(8,128)S(1)}, u32[]{:S(2)}, u32[]{:S(2)}) collective-permute-start(f32[8,512]{1,0:T(8,128)S(1)} %reshape.75), channel_id=1, source_target_pairs={{0,4},{4,0},{1,5},{5,1},{2,6},{6,2},{3,7},{7,3},{8,12},{12,8},{9,1... | collective-permute-start | bytes 49160 | tf_op jit(solution)/shard_map/ppermute | solution.py:21
  90.6 2.9 %collective-permute-start.3 = (f32[8,512]{1,0:T(8,128)S(1)}, f32[8,512]{1,0:T(8,128)S(1)}, u32[]{:S(2)}, u32[]{:S(2)}) collective-permute-start(f32[8,512]{1,0:T(8,128)S(1)} %reshape.77), channel_id=1, source_target_pairs={{4,0},{0,4},{5,1},{1,5},{6,2},{2,6},{7,3},{3,7},{12,8},{8,12},{13,... | collective-permute-start | bytes 49160 | tf_op jit(solution)/shard_map/ppermute | solution.py:21
  103.6 21.8 %all-to-all-start.1 = ((f32[16,8,1024]{2,1,0:T(8,128)}), f32[16,8,1024]{2,1,0:T(8,128)S(1)}, u32[]{:S(2)}, u32[]{:S(2)}) async-start(f32[16,8,1024]{2,1,0:T(8,128)} %bitcast.103), calls=%async_computation.1 | async-start | bytes 1048576 | tf_op jit(solution)/shard_map/all_to_all | solution.py:269
  125.3 1.2 copy-start.2
